TPU v7x, 32 devices: a whole 2x2x4 slice. The times are simulated.
32 devices in a mesh: row: 8 (over z, y), col: 4 (over x, core).
Axes of the slice: x: 2, y: 2, z: 4, core: 2. Of those that a mesh axis runs over, the one named last changes fastest.
Arguments:
- embeddings: bfloat16 [5, 192, 2048], P(None, None, ('row', 'col')), may hold values from -6 to 6
- scale_weights: float32 [5], replicated, may hold values from 0.1 to 0.5
- vectors: bfloat16 [32, 2048], P(None, ('row', 'col')), may hold values from -6 to 6
Outputs:
- product: float32 [32, 2048], P(None, ('row', 'col'))
All inputs are finite; a program needn't handle non-finite values.
Results may differ from a plain program's by a relative error of at most 0.011.
Values may be sent and summed in bfloat16 or wider, within the bound.
A program may use at most 64 MiB of HBM per device.

v0:
```python
import math

import jax
import jax.numpy as jnp
from jax import lax
from jax.sharding import PartitionSpec as P

SHARP = 3.5


def prepare(embeddings, scale_weights):
    values = embeddings.astype(jnp.float32)
    units = values * lax.rsqrt(jnp.sum(values * values, axis=1, keepdims=True) + 1e-06)
    unit = lax.optimization_barrier(units.astype(jnp.bfloat16))
    weighted = (scale_weights[:, None, None] * unit.astype(jnp.float32)).astype(jnp.bfloat16)
    segments = embeddings.shape[2]
    return (weighted.reshape(-1, segments), unit.reshape(-1, segments))


def tile_terms(row_panel, column_panel, column_vectors, row_ids, column_ids, sharpness):
    cosine = lax.dot_general(
        row_panel, column_panel, (((0,), (0,)), ((), ())), preferred_element_type=jnp.float32
    )
    affinity = jnp.where(
        row_ids[:, None] == column_ids[None, :], jnp.zeros_like(cosine), jnp.exp(sharpness * cosine)
    )
    degree = jnp.sum(affinity, axis=1)
    numerator = lax.dot_general(
        column_vectors,
        affinity.astype(jnp.bfloat16),
        (((1,), (1,)), ((), ())),
        preferred_element_type=jnp.float32,
    )
    return (numerator, degree)


def blocked(row_panel, column_panel, column_vectors, row_ids, column_ids, sharpness):
    width = column_panel.shape[1]
    stride = math.gcd(width, 512)
    numerator = jnp.zeros((column_vectors.shape[0], row_panel.shape[1]), jnp.float32)
    degree = jnp.zeros((row_panel.shape[1],), jnp.float32)
    for offset in range(0, width, stride):
        extra_numerator, extra_degree = tile_terms(
            row_panel,
            column_panel[:, offset : offset + stride],
            column_vectors[:, offset : offset + stride],
            row_ids,
            column_ids[offset : offset + stride],
            sharpness,
        )
        numerator = numerator + extra_numerator
        degree = degree + extra_degree
    return (numerator, degree)


def shards(embeddings, scale_weights, vectors):
    segments = embeddings.shape[2]
    col_count = lax.axis_size("col")
    row_index = lax.axis_index("row")
    col_index = lax.axis_index("col")
    sharpness = SHARP * math.sqrt(embeddings.shape[1])
    weighted, unit = prepare(embeddings, scale_weights)

    def positions_of(panel):
        return jnp.arange(panel.shape[1], dtype=jnp.int32)

    own_panel = lax.all_gather(weighted, "col", axis=1, tiled=True)
    own_ids = row_index * (col_count * segments) + positions_of(own_panel)
    partner_panel, partner_vectors = (
        lax.all_gather(unit, "row", axis=1, tiled=True),
        lax.all_gather(vectors, "row", axis=1, tiled=True),
    )
    positions = positions_of(partner_panel)
    numerator, degree = blocked(
        own_panel,
        partner_panel,
        partner_vectors,
        own_ids,
        (positions // segments * col_count + col_index) * segments + positions % segments,
        sharpness,
    )
    numerator, degree = (
        lax.psum_scatter(numerator, "col", scatter_dimension=1, tiled=True),
        lax.psum_scatter(degree, "col", scatter_dimension=0, tiled=True),
    )
    return numerator / degree[None, :]


def solution(mesh):
    placed = (P(None, None, ("row", "col")), P(), P(None, ("row", "col")))
    return jax.shard_map(
        shards, mesh=mesh, in_specs=placed, out_specs=P(None, ("row", "col")), check_vma=False
    )
```

profile of v0, /device:TPU:0, one launch (start us, length us, event | category | flops | bytes accessed | tf_op | source)
XLA Modules:
  0.0 111.4 jit_solution(14193638312619526555)
XLA Ops:
  6.5 0.0 copy-start
  6.5 0.0 reduce-scatter.4.cloned.1.call-start
  6.5 1.1 fusion.2
  7.7 0.0 copy-done
  7.7 0.1 fusion.3
  7.8 0.1 copy.8
  7.9 0.2 reshape.43
  8.1 0.0 copy-start.2
  8.1 34.6 %all_gather.10 = bf16[960,512]{0,1:T(8,128)(2,1)S(1)} all-gather(bf16[960,64]{0,1:T(8,128)(2,1)S(1)} %reshape.43), channel_id=1, replica_groups=mesh['row'=8,'col'=4] {'row'}, dimensions={1}, use_global_device_ids=true | all-gather | bytes 1105920 | tf_op jit(solution)/shard_map/all_gather | solution.py:70
  42.7 0.0 copy-done.2
  42.7 0.1 multiply_convert_fusion
  42.8 0.1 copy.7
  42.9 0.2 reshape.42
  43.0 7.2 %all_gather.9 = bf16[960,256]{0,1:T(8,128)(2,1)S(1)} all-gather(bf16[960,64]{0,1:T(8,128)(2,1)S(1)} %reshape.42), channel_id=1, replica_groups=mesh['row'=8,'col'=4] {'col'}, dimensions={1}, use_global_device_ids=true | all-gather | bytes 614400 | tf_op jit(solution)/shard_map/all_gather | solution.py:67
  50.2 0.0 copy-start.1
  50.2 0.7 copy-done.1
  50.9 30.5 %all-gather = bf16[8,64,32]{1,2,0:T(8,128)(2,1)S(1)} all-gather(bf16[1,64,32]{1,2,0:T(8,128)(2,1)S(1)} %bitcast.20), channel_id=1, replica_groups=mesh['row'=8,'col'=4] {'row'}, dimensions={0}, use_global_device_ids=true | all-gather | bytes 36864 | tf_op jit(solution)/shard_map/all_gather | solution.py:71
  81.5 0.1 reshape.45
  81.6 0.6 fusion.16
  82.2 0.2 convolution_bitcast_fusion
  82.4 0.7 copy.10
  83.1 0.0 reduce-scatter.4.cloned.1.call-update
  83.1 0.0 copy-start.3
  83.2 0.6 copy-done.3
  83.8 0.6 dynamic-slice
  85.0 5.7 %all-reduce = f32[256]{0:T(256)S(1)} all-reduce(f32[256]{0:T(256)S(1)} %get-tuple-element.5), channel_id=3, replica_groups=mesh['row'=8,'col'=4] {'col'}, use_global_device_ids=true, to_apply=%region_3.4.clone | all-reduce | flops 256 | bytes 2048
  90.7 0.1 dynamic-slice.1
  90.8 12.3 %reduce-scatter.4.cloned.1.call-done = f32[64,32]{1,0:T(8,128)} async-done(((f32[256,32]{1,0:T(8,128)}), f32[64,32]{1,0:T(8,128)}) %reduce-scatter.4.cloned.1.call-update) | async-done | bytes 8208
  103.1 0.8 copy.11
  103.9 0.6 broadcast_divide_fusion
  (4 shorter events, 0.0 us)
Async XLA Ops:
  6.5 1.1 %copy-start = (bf16[5,192,64]{1,2,0:T(8,128)(2,1)S(1)}, bf16[5,192,64]{1,2,0:T(8,128)(2,1)}, u32[]{:S(2)}) copy-start(bf16[5,192,64]{1,2,0:T(8,128)(2,1)} %param.3) | copy-start | bytes 368644
  6.5 96.5 %reduce-scatter.4.cloned.1.call-start = ((), (), s32[]{:S(2)}) async-start(), calls=%async_computation.1 | async-start | bytes 163840
  8.1 34.6 %copy-start.2 = (f32[5]{0:T(128)S(1)}, f32[5]{0:T(128)}, u32[]{:S(2)}) copy-start(f32[5]{0:T(128)} %param.4) | copy-start | bytes 64
  50.2 0.7 copy-start.1
  83.1 0.7 copy-start.3
Sparse Core Ops, SparseCore 0:
  83.3 19.7 reduce-scatter.3
where the time goes:
time: 112 us; the launch traced here: 111 us
  blocking collectives  78 us (70%)
  between operations  14.1 us (13%)
  waiting for transfers between devices  12.3 us (11%)
  local copies, waits for them, and re-layouts  4.23 us (4%)
  other arithmetic  1.94 us (2%)
    all_gather x1, blocking collectives, shards(): lax.all_gather(unit, 'row', axis=1, tiled=True)  34.6 us
    all_gather x1, blocking collectives, shards(): lax.all_gather(vectors, 'row', axis=1, tiled=True)  30.5 us
    unnamed x2, waiting for transfers between devices  12.3 us
    all_gather x1, blocking collectives, shards(): own_panel = lax.all_gather(weighted, 'col', axis=1, tiled=True)  7.17 us
    unnamed x1, blocking collectives  5.67 us
    unnamed x13, local copies, waits for them, and re-layouts  3.68 us
  transfers between devices with their start and end apart: 1, of which 1 were waited for; matrix products, arithmetic and copies ran while one was open for 1% of the time, Pallas kernels for 0%

commit v1 on v0

v1 whole, which is shorter than its diff:
```python
import functools
import math

import jax
import jax.numpy as jnp
from jax import lax
from jax.experimental import pallas as pl
from jax.experimental.pallas import tpu as pltpu
from jax.sharding import PartitionSpec as P

SHARP = 3.5
LANES = 128
CORES = 2
CHUNKS = 2
MESH = pl.DeviceIdType.MESH


def kernel(
    plan, emb_ref, scale_ref, vec_ref, out_ref, rows, cols, partial, landed,
    line_send, line_recv, own_send, own_recv, pair_send, pair_recv, part_send, part_recv,
):
    line, near, wide, width = plan
    scales, dim, segments = emb_ref.shape
    vecs = vec_ref.shape[0]
    feats = scales * dim
    row, col = lax.axis_index("row"), lax.axis_index("col")
    z, q = row // near, lax.rem(row, near)
    me = q * wide + col
    partner = col + 1 - 2 * lax.rem(col, CORES)

    def at(other_z, other_q, other_col):
        return (other_z * near + other_q, other_col)

    barrier = pltpu.get_barrier_semaphore()
    greeted = 0
    for step in (1, line - 1):
        if line > 1:
            pl.semaphore_signal(
                barrier, inc=1, device_id=at(lax.rem(z + step, line), q, col), device_id_type=MESH
            )
            greeted += 1
    for dq in range(near):
        for dc in range(wide):
            if dq or dc:
                pl.semaphore_signal(
                    barrier,
                    inc=1,
                    device_id=at(z, lax.rem(q + dq, near), lax.rem(col + dc, wide)),
                    device_id_type=MESH,
                )
                greeted += 1

    units, weights = [], []
    for s in range(scales):
        values = emb_ref[s].astype(jnp.float32)
        unit = values * lax.rsqrt(jnp.sum(values * values, axis=0, keepdims=True) + 1e-06)
        unit = unit.astype(jnp.bfloat16)
        units.append(unit)
        weights.append((scale_ref[s] * unit.astype(jnp.float32)).astype(jnp.bfloat16))
    rest = width - feats - vecs
    units += [vec_ref[...], jnp.ones((rest, segments), jnp.bfloat16)]
    weights.append(jnp.zeros((width - feats, segments), jnp.bfloat16))
    cols[z] = jnp.concatenate(units, axis=0).T
    rows[me] = jnp.concatenate(weights, axis=0).T
    pl.semaphore_wait(barrier, greeted)

    size = segments // CHUNKS

    def line_copy(up, step, chunk):
        block = z - step if up else z + step
        there = z + 1 if up else z - 1
        piece = cols.at[jnp.clip(block, 0, line - 1), pl.ds(chunk * size, size)]
        k = int(up)
        copy = pltpu.make_async_remote_copy(
            src_ref=piece,
            dst_ref=piece,
            send_sem=line_send.at[k, step, chunk],
            recv_sem=line_recv.at[k, step, chunk],
            device_id=at(jnp.clip(there, 0, line - 1), q, col),
            device_id_type=MESH,
        )
        sends = (z - step >= 0) & (z < line - 1) if up else (z + step <= line - 1) & (z > 0)
        return copy, sends

    def line_start(up, step, chunk):
        copy, sends = line_copy(up, step, chunk)
        pl.when(sends)(copy.start)

    def line_arrive(up, step, chunk):
        block = z - 1 - step if up else z + 1 + step
        piece = cols.at[jnp.clip(block, 0, line - 1), pl.ds(chunk * size, size)]
        gets = (z - 1 - step >= 0) if up else (z + 1 + step <= line - 1)

        @pl.when(gets)
        def _():
            pltpu.make_async_remote_copy(
                src_ref=piece,
                dst_ref=piece,
                send_sem=line_send.at[int(up), step, chunk],
                recv_sem=line_recv.at[int(up), step, chunk],
                device_id=at(jnp.clip(z - 1 if up else z + 1, 0, line - 1), q, col),
                device_id_type=MESH,
            ).wait_recv()

    hops = [(dq, dc) for dq in range(near) for dc in range(0, wide, CORES)]
    hops.sort(key=lambda hop: (hop[0] != 0) + (hop[1] != 0))

    def own_copy(k, slot, to):
        return pltpu.make_async_remote_copy(
            src_ref=rows.at[slot],
            dst_ref=rows.at[slot],
            send_sem=own_send.at[k],
            recv_sem=own_recv.at[k],
            device_id=to,
            device_id_type=MESH,
        )

    def source(k, column):
        dq, dc = hops[k]
        return lax.rem(q - dq + near, near) * wide + lax.rem(column - dc + wide, wide)

    def pair_copy(k, slot):
        return pltpu.make_async_remote_copy(
            src_ref=rows.at[slot],
            dst_ref=rows.at[slot],
            send_sem=pair_send.at[k],
            recv_sem=pair_recv.at[k],
            device_id=at(z, q, partner),
            device_id_type=MESH,
        )

    def hop_to(k):
        dq, dc = hops[k]
        return at(z, lax.rem(q + dq, near), lax.rem(col + dc, wide))

    for chunk in range(CHUNKS):
        for up in (True, False):
            if line > 1:
                line_start(up, 0, chunk)
    for k in range(1, len(hops)):
        own_copy(k, me, hop_to(k)).start()
    pair_copy(0, me).start()

    def plane_pass(k):
        slot = source(k, col)
        own_copy(k, slot, hop_to(k)).wait_recv()
        pair_copy(k, slot).start()

    todo = list(range(1, len(hops)))
    each = -(-len(todo) // max(line - 1, 1))
    for step in range(line - 1):
        for chunk in range(CHUNKS):
            for up in (True, False):
                line_arrive(up, step, chunk)
                if step + 1 < line - 1:
                    line_start(up, step + 1, chunk)
        for k in todo[step * each : (step + 1) * each]:
            plane_pass(k)
    for k in todo[(line - 1) * each :]:
        plane_pass(k)
    for k in range(len(hops)):
        pair_copy(k, source(k, partner)).wait_recv()

    sharpness = SHARP * math.sqrt(dim)
    count = line * segments
    columns = cols[...].reshape(count, width)
    base = feats // LANES * LANES
    tail = columns[:, base:]
    positions = lax.broadcasted_iota(jnp.int32, (1, count), 1)
    column_ids = (positions // segments * (near * wide) + me) * segments + positions % segments
    for step in range(1, near + 1):
        other = lax.rem(q + step, near)
        first = other * wide
        panel = rows[pl.ds(first, wide)].reshape(wide * segments, width)
        cosine = lax.dot_general(
            panel, columns, (((1,), (1,)), ((), ())), preferred_element_type=jnp.float32
        )
        row_ids = (z * near * wide + first) * segments + lax.broadcasted_iota(
            jnp.int32, (wide * segments, 1), 0
        )
        affinity = jnp.where(
            row_ids == column_ids, jnp.zeros_like(cosine), jnp.exp(sharpness * cosine)
        )
        sums = lax.dot_general(
            affinity.astype(jnp.bfloat16), tail, (((1,), (0,)), ((), ())),
            preferred_element_type=jnp.float32,
        )
        partial[pl.ds(first, wide)] = sums.reshape(wide, segments, width - base)

        for dc in range(wide):
            dq = step % near
            if dq or dc:
                k = dq * wide + dc
                to = lax.rem(col + dc, wide)
                pltpu.make_async_remote_copy(
                    src_ref=partial.at[first + to],
                    dst_ref=landed.at[k],
                    send_sem=part_send.at[k],
                    recv_sem=part_recv.at[k],
                    device_id=at(z, other, to),
                    device_id_type=MESH,
                ).start()

    def part_copy(k):
        dq, dc = k // wide, k % wide
        other, to = lax.rem(q + dq, near), lax.rem(col + dc, wide)
        return pltpu.make_async_remote_copy(
            src_ref=partial.at[other * wide + to],
            dst_ref=landed.at[k],
            send_sem=part_send.at[k],
            recv_sem=part_recv.at[k],
            device_id=at(z, other, to),
            device_id_type=MESH,
        )

    total = partial[me]
    for k in range(1, near * wide):
        part_copy(k).wait_recv()
        total = total + landed[k]
    total = total.T
    low = feats - base
    out_ref[...] = total[low : low + vecs] / total[low + vecs : low + vecs + 1]

    for k in range(1, near * wide):
        part_copy(k).wait_send()
    for k in range(len(hops)):
        if k:
            own_copy(k, me, hop_to(k)).wait_send()
        pair_copy(k, source(k, col)).wait_send()
    for step in range(line - 1):
        for chunk in range(CHUNKS):
            for up in (True, False):
                copy, sends = line_copy(up, step, chunk)
                pl.when(sends)(copy.wait_send)


def shards(shape, embeddings, scale_weights, vectors):
    row_count, wide = shape
    near = math.gcd(row_count, 2)
    line = row_count // near
    scales, dim, segments = embeddings.shape
    vecs = vectors.shape[0]
    feats = scales * dim
    width = -(-(feats + vecs + 1) // LANES) * LANES
    plane = near * wide
    base = feats // LANES * LANES
    hops = near * wide // CORES
    steps = max(line - 1, 1)
    dma = pltpu.SemaphoreType.DMA
    return pl.pallas_call(
        functools.partial(kernel, (line, near, wide, width)),
        out_shape=jax.ShapeDtypeStruct((vecs, segments), jnp.float32),
        in_specs=[
            pl.BlockSpec(memory_space=pltpu.VMEM),
            pl.BlockSpec(memory_space=pltpu.SMEM),
            pl.BlockSpec(memory_space=pltpu.VMEM),
        ],
        out_specs=pl.BlockSpec(memory_space=pltpu.VMEM),
        scratch_shapes=[
            pltpu.VMEM((plane, segments, width), jnp.bfloat16),
            pltpu.VMEM((line, segments, width), jnp.bfloat16),
            pltpu.VMEM((plane, segments, width - base), jnp.float32),
            pltpu.VMEM((plane, segments, width - base), jnp.float32),
            dma((2, steps, CHUNKS)),
            dma((2, steps, CHUNKS)),
            dma((hops,)),
            dma((hops,)),
            dma((hops,)),
            dma((hops,)),
            dma((plane,)),
            dma((plane,)),
        ],
        compiler_params=pltpu.CompilerParams(
            collective_id=0, has_side_effects=True, vmem_limit_bytes=56 * 1024 * 1024
        ),
    )(embeddings, scale_weights, vectors)


def solution(mesh):
    placed = (P(None, None, ("row", "col")), P(), P(None, ("row", "col")))
    return jax.shard_map(
        functools.partial(shards, (mesh.shape["row"], mesh.shape["col"])),
        mesh=mesh, in_specs=placed, out_specs=P(None, ("row", "col")), check_vma=False,
    )
```

time: 112 us -> 28.2 us (0.25)
  blocking collectives: 78 us -> 0 us
  Pallas kernels: 0 us -> 24.9 us
  between operations: 14.1 us -> 0.01 us
  waiting for transfers between devices: 12.3 us -> 0 us
  other arithmetic: 1.94 us -> 0 us
  local copies, waits for them, and re-layouts: 4.23 us -> 3.08 us
    all_gather x3 -> x0, blocking collectives: 72.3 us -> none  [the longest x1 34.6 us: shards(): lax.all_gather(unit, 'row', axis=1, tiled=True)]
    pallas_call x0 -> x1, Pallas kernels: none -> 24.9 us  [shards(): pl.pallas_call(functools.partial(kernel, (line, near, wide, width)), out_...]
    unnamed x2 -> x0, waiting for transfers between devices: 12.3 us -> none
    unnamed x1 -> x0, blocking collectives: 5.67 us -> none
    unnamed x13 -> x2, local copies, waits for them, and re-layouts: 3.68 us -> 3.08 us
  transfers between devices with their start and end apart: 1 -> 0, of which waited for: 1 -> 0; matrix products, arithmetic and copies ran while one was open for 1% -> 0% of each run, Pallas kernels for 0% -> 0%
where the time goes in v1:
time: 28.2 us; the launch traced here: 28 us
  Pallas kernels  24.9 us (88%)
  local copies, waits for them, and re-layouts  3.08 us (11%)
    pallas_call x1, Pallas kernels, shards(): pl.pallas_call(functools.partial(kernel, (line, near, wide, width)), out_...  24.9 us
    unnamed x2, local copies, waits for them, and re-layouts  3.08 us

profile of v1, /device:TPU:0, one launch (start us, length us, event | category | flops | bytes accessed | tf_op | source)
XLA Modules:
  0.0 28.0 jit_solution(13102513357725966408)
XLA Ops:
  0.0 1.8 %copy.4.emb_ref = bf16[5,192,64]{2,1,0:T(8,128)(2,1)} copy(bf16[5,192,64]{1,2,0:T(8,128)(2,1)} %param.3) | data formatting | bytes 245760 | tf_op args[0]
  1.8 24.9 %shard_map.37 = f32[32,64]{1,0:T(8,128)} custom-call(bf16[5,192,64]{2,1,0:T(8,128)(2,1)} %copy.4.emb_ref, f32[5]{0:T(128)} %scale_ref.1, bf16[32,64]{1,0:T(8,128)(2,1)} %vec_ref.1), custom_call_target="tpu_custom_call" | custom-call | tf_op jit(solution)/shard_map/pallas_call | solution.py:250
  26.7 1.3 %copy.6 = f32[32,64]{1,0:T(8,128)} copy(f32[32,64]{1,0:T(8,128)} %shard_map.37) | data formatting | bytes 16384

commit v2 on v1

--- a/solution.py
+++ b/solution.py
@@ -20,7 +20,7 @@
     line_send, line_recv, own_send, own_recv, pair_send, pair_recv, part_send, part_recv,
 ):
     line, near, wide, width = plan
-    scales, dim, segments = emb_ref.shape
+    scales, segments, dim = emb_ref.shape
     vecs = vec_ref.shape[0]
     feats = scales * dim
     row, col = lax.axis_index("row"), lax.axis_index("col")
@@ -50,18 +50,21 @@
                 )
                 greeted += 1
 
-    units, weights = [], []
+    whole = dim // LANES * LANES
+    units, unit_rests, weights, weight_rests = [], [], [], []
     for s in range(scales):
         values = emb_ref[s].astype(jnp.float32)
-        unit = values * lax.rsqrt(jnp.sum(values * values, axis=0, keepdims=True) + 1e-06)
+        unit = values * lax.rsqrt(jnp.sum(values * values, axis=1, keepdims=True) + 1e-06)
         unit = unit.astype(jnp.bfloat16)
-        units.append(unit)
-        weights.append((scale_ref[s] * unit.astype(jnp.float32)).astype(jnp.bfloat16))
-    rest = width - feats - vecs
-    units += [vec_ref[...], jnp.ones((rest, segments), jnp.bfloat16)]
-    weights.append(jnp.zeros((width - feats, segments), jnp.bfloat16))
-    cols[z] = jnp.concatenate(units, axis=0).T
-    rows[me] = jnp.concatenate(weights, axis=0).T
+        weighted = (scale_ref[s] * unit.astype(jnp.float32)).astype(jnp.bfloat16)
+        units.append(unit[:, :whole])
+        unit_rests.append(unit[:, whole:])
+        weights.append(weighted[:, :whole])
+        weight_rests.append(weighted[:, whole:])
+    ones = jnp.ones((segments, width - feats - vecs), jnp.bfloat16)
+    zeros = jnp.zeros((segments, width - feats), jnp.bfloat16)
+    cols[z] = jnp.concatenate(units + unit_rests + [vec_ref[...].T, ones], axis=1)
+    rows[me] = jnp.concatenate(weights + weight_rests + [zeros], axis=1)
     pl.semaphore_wait(barrier, greeted)
 
     size = segments // CHUNKS
@@ -273,7 +276,7 @@
         compiler_params=pltpu.CompilerParams(
             collective_id=0, has_side_effects=True, vmem_limit_bytes=56 * 1024 * 1024
         ),
-    )(embeddings, scale_weights, vectors)
+    )(jnp.swapaxes(embeddings, 1, 2), scale_weights, vectors)
 
 
 def solution(mesh):

time: 28.2 us -> 26.4 us (0.936)
  local copies, waits for them, and re-layouts: 3.08 us -> 1.32 us
    unnamed x2 -> x1, local copies, waits for them, and re-layouts: 3.08 us -> 1.32 us
where the time goes in v2:
time: 26.4 us; the launch traced here: 26.2 us
  Pallas kernels  24.9 us (94%)
  local copies, waits for them, and re-layouts  1.32 us (5%)
    pallas_call x1, Pallas kernels, shards(): pl.pallas_call(functools.partial(kernel, (line, near, wide, width)), out_...  24.9 us
    unnamed x1, local copies, waits for them, and re-layouts  1.32 us

profile of v2, /device:TPU:0, one launch (start us, length us, event | category | flops | bytes accessed | tf_op | source)
XLA Modules:
  0.0 26.2 jit_solution(2588584789508546922)
XLA Ops:
  0.0 24.9 %shard_map.37 = f32[32,64]{1,0:T(8,128)} custom-call(bf16[5,64,192]{2,1,0:T(8,128)(2,1)} %bitcast.1, f32[5]{0:T(128)} %scale_ref.1, bf16[32,64]{1,0:T(8,128)(2,1)} %vec_ref.1), custom_call_target="tpu_custom_call" | custom-call | tf_op jit(solution)/shard_map/pallas_call | solution.py:253
  24.9 1.3 %copy.5 = f32[32,64]{1,0:T(8,128)} copy(f32[32,64]{1,0:T(8,128)} %shard_map.37) | data formatting | bytes 16384

commit v3 on v2

--- a/solution.py
+++ b/solution.py
@@ -11,12 +11,12 @@
 SHARP = 3.5
 LANES = 128
 CORES = 2
-CHUNKS = 2
+CHUNKS = 4
 MESH = pl.DeviceIdType.MESH
 
 
 def kernel(
-    plan, emb_ref, scale_ref, vec_ref, out_ref, rows, cols, partial, landed,
+    plan, emb_ref, scale_ref, vec_ref, out_ref, values_ref, load_sem, rows, cols, partial, landed,
     line_send, line_recv, own_send, own_recv, pair_send, pair_recv, part_send, part_recv,
 ):
     line, near, wide, width = plan
@@ -31,29 +31,30 @@
     def at(other_z, other_q, other_col):
         return (other_z * near + other_q, other_col)
 
+    load = pltpu.make_async_copy(emb_ref, values_ref, load_sem)
+    load.start()
     barrier = pltpu.get_barrier_semaphore()
-    greeted = 0
-    for step in (1, line - 1):
-        if line > 1:
-            pl.semaphore_signal(
-                barrier, inc=1, device_id=at(lax.rem(z + step, line), q, col), device_id_type=MESH
-            )
-            greeted += 1
-    for dq in range(near):
-        for dc in range(wide):
-            if dq or dc:
-                pl.semaphore_signal(
-                    barrier,
-                    inc=1,
-                    device_id=at(z, lax.rem(q + dq, near), lax.rem(col + dc, wide)),
-                    device_id_type=MESH,
-                )
-                greeted += 1
+    greeted = (z > 0).astype(jnp.int32) + (z < line - 1).astype(jnp.int32)
+
+    def greet(device):
+        pl.semaphore_signal(barrier, inc=1, device_id=device, device_id_type=MESH)
+
+    pl.when(z > 0)(lambda: greet(at(z - 1, q, col)))
+    pl.when(z < line - 1)(lambda: greet(at(z + 1, q, col)))
+    greet(at(z, q, partner))
+    greeted = greeted + 1
+    for dc in range(CORES, wide, CORES):
+        greet(at(z, q, lax.rem(col + dc, wide)))
+        greeted = greeted + 1
+    if near > 1:
+        greet(at(z, 1 - q, col))
+        greeted = greeted + 1
+    load.wait()
 
     whole = dim // LANES * LANES
     units, unit_rests, weights, weight_rests = [], [], [], []
     for s in range(scales):
-        values = emb_ref[s].astype(jnp.float32)
+        values = values_ref[s].astype(jnp.float32)
         unit = values * lax.rsqrt(jnp.sum(values * values, axis=1, keepdims=True) + 1e-06)
         unit = unit.astype(jnp.bfloat16)
         weighted = (scale_ref[s] * unit.astype(jnp.float32)).astype(jnp.bfloat16)
@@ -106,7 +107,7 @@
             ).wait_recv()
 
     hops = [(dq, dc) for dq in range(near) for dc in range(0, wide, CORES)]
-    hops.sort(key=lambda hop: (hop[0] != 0) + (hop[1] != 0))
+    pairs = wide // CORES
 
     def own_copy(k, slot, to):
         return pltpu.make_async_remote_copy(
@@ -134,19 +135,26 @@
 
     def hop_to(k):
         dq, dc = hops[k]
-        return at(z, lax.rem(q + dq, near), lax.rem(col + dc, wide))
+        return at(z, 1 - q, col) if dq else at(z, q, lax.rem(col + dc, wide))
+
+    def relay(k):
+        if near > 1:
+            own_copy(k + pairs, source(k, col), hop_to(k + pairs)).start()
 
     for chunk in range(CHUNKS):
         for up in (True, False):
             if line > 1:
                 line_start(up, 0, chunk)
-    for k in range(1, len(hops)):
+    for k in range(1, pairs):
         own_copy(k, me, hop_to(k)).start()
+    relay(0)
     pair_copy(0, me).start()
 
     def plane_pass(k):
         slot = source(k, col)
         own_copy(k, slot, hop_to(k)).wait_recv()
+        if k < pairs:
+            relay(k)
         pair_copy(k, slot).start()
 
     todo = list(range(1, len(hops)))
@@ -188,7 +196,7 @@
             affinity.astype(jnp.bfloat16), tail, (((1,), (0,)), ((), ())),
             preferred_element_type=jnp.float32,
         )
-        partial[pl.ds(first, wide)] = sums.reshape(wide, segments, width - base)
+        partial[pl.ds(first, wide)] = sums.astype(jnp.bfloat16).reshape(wide, segments, width - base)
 
         for dc in range(wide):
             dq = step % near
@@ -216,10 +224,10 @@
             device_id_type=MESH,
         )
 
-    total = partial[me]
+    total = partial[me].astype(jnp.float32)
     for k in range(1, near * wide):
         part_copy(k).wait_recv()
-        total = total + landed[k]
+        total = total + landed[k].astype(jnp.float32)
     total = total.T
     low = feats - base
     out_ref[...] = total[low : low + vecs] / total[low + vecs : low + vecs + 1]
@@ -254,16 +262,18 @@
         functools.partial(kernel, (line, near, wide, width)),
         out_shape=jax.ShapeDtypeStruct((vecs, segments), jnp.float32),
         in_specs=[
-            pl.BlockSpec(memory_space=pltpu.VMEM),
+            pl.BlockSpec(memory_space=pl.ANY),
             pl.BlockSpec(memory_space=pltpu.SMEM),
             pl.BlockSpec(memory_space=pltpu.VMEM),
         ],
         out_specs=pl.BlockSpec(memory_space=pltpu.VMEM),
         scratch_shapes=[
+            pltpu.VMEM((scales, segments, dim), jnp.bfloat16),
+            dma,
             pltpu.VMEM((plane, segments, width), jnp.bfloat16),
             pltpu.VMEM((line, segments, width), jnp.bfloat16),
-            pltpu.VMEM((plane, segments, width - base), jnp.float32),
-            pltpu.VMEM((plane, segments, width - base), jnp.float32),
+            pltpu.VMEM((plane, segments, width - base), jnp.bfloat16),
+            pltpu.VMEM((plane, segments, width - base), jnp.bfloat16),
             dma((2, steps, CHUNKS)),
             dma((2, steps, CHUNKS)),
             dma((hops,)),

time: 26.4 us -> 24 us (0.909)
  Pallas kernels: 24.9 us -> 22.3 us
    pallas_call x1, Pallas kernels: 24.9 us -> 22.3 us  [shards(): pl.pallas_call(functools.partial(kernel, (line, near, wide, width)), out_...]
where the time goes in v3:
time: 24 us; the launch traced here: 23.7 us
  Pallas kernels  22.3 us (93%)
  local copies, waits for them, and re-layouts  1.32 us (6%)
    pallas_call x1, Pallas kernels, shards(): pl.pallas_call(functools.partial(kernel, (line, near, wide, width)), out_...  22.3 us
    unnamed x1, local copies, waits for them, and re-layouts  1.32 us

profile of v3, /device:TPU:0, one launch (start us, length us, event | category | flops | bytes accessed | tf_op | source)
XLA Modules:
  0.0 23.7 jit_solution(18439679609115606451)
XLA Ops:
  0.0 22.3 %shard_map.37 = f32[32,64]{1,0:T(8,128)} custom-call(bf16[5,64,192]{2,1,0:T(8,128)(2,1)} %bitcast.1, f32[5]{0:T(128)} %scale_ref.1, bf16[32,64]{1,0:T(8,128)(2,1)} %vec_ref.1), custom_call_target="tpu_custom_call" | custom-call | tf_op jit(solution)/shard_map/pallas_call | solution.py:261
  22.3 1.3 %copy.5 = f32[32,64]{1,0:T(8,128)} copy(f32[32,64]{1,0:T(8,128)} %shard_map.37) | data formatting | bytes 16384

commit v4 on v3

--- a/solution.py
+++ b/solution.py
@@ -12,6 +12,7 @@
 LANES = 128
 CORES = 2
 CHUNKS = 4
+PIECES = 2
 MESH = pl.DeviceIdType.MESH
 
 
@@ -109,12 +110,15 @@
     hops = [(dq, dc) for dq in range(near) for dc in range(0, wide, CORES)]
     pairs = wide // CORES
 
-    def own_copy(k, slot, to):
+    part = segments // PIECES
+
+    def own_copy(k, piece, slot, to):
+        block = rows.at[slot, pl.ds(piece * part, part)]
         return pltpu.make_async_remote_copy(
-            src_ref=rows.at[slot],
-            dst_ref=rows.at[slot],
-            send_sem=own_send.at[k],
-            recv_sem=own_recv.at[k],
+            src_ref=block,
+            dst_ref=block,
+            send_sem=own_send.at[k, piece],
+            recv_sem=own_recv.at[k, piece],
             device_id=to,
             device_id_type=MESH,
         )
@@ -123,12 +127,13 @@
         dq, dc = hops[k]
         return lax.rem(q - dq + near, near) * wide + lax.rem(column - dc + wide, wide)
 
-    def pair_copy(k, slot):
+    def pair_copy(k, piece, slot):
+        block = rows.at[slot, pl.ds(piece * part, part)]
         return pltpu.make_async_remote_copy(
-            src_ref=rows.at[slot],
-            dst_ref=rows.at[slot],
-            send_sem=pair_send.at[k],
-            recv_sem=pair_recv.at[k],
+            src_ref=block,
+            dst_ref=block,
+            send_sem=pair_send.at[k, piece],
+            recv_sem=pair_recv.at[k, piece],
             device_id=at(z, q, partner),
             device_id_type=MESH,
         )
@@ -137,40 +142,45 @@
         dq, dc = hops[k]
         return at(z, 1 - q, col) if dq else at(z, q, lax.rem(col + dc, wide))
 
-    def relay(k):
+    def relay(k, piece):
         if near > 1:
-            own_copy(k + pairs, source(k, col), hop_to(k + pairs)).start()
+            own_copy(k + pairs, piece, source(k, col), hop_to(k + pairs)).start()
 
     for chunk in range(CHUNKS):
         for up in (True, False):
             if line > 1:
                 line_start(up, 0, chunk)
-    for k in range(1, pairs):
-        own_copy(k, me, hop_to(k)).start()
-    relay(0)
-    pair_copy(0, me).start()
-
-    def plane_pass(k):
+    for piece in range(PIECES):
+        for k in range(1, pairs):
+            own_copy(k, piece, me, hop_to(k)).start()
+        relay(0, piece)
+        pair_copy(0, piece, me).start()
+
+    def plane_pass(k, piece):
         slot = source(k, col)
-        own_copy(k, slot, hop_to(k)).wait_recv()
+        own_copy(k, piece, slot, hop_to(k)).wait_recv()
         if k < pairs:
-            relay(k)
-        pair_copy(k, slot).start()
-
-    todo = list(range(1, len(hops)))
-    each = -(-len(todo) // max(line - 1, 1))
-    for step in range(line - 1):
-        for chunk in range(CHUNKS):
-            for up in (True, False):
-                line_arrive(up, step, chunk)
-                if step + 1 < line - 1:
-                    line_start(up, step + 1, chunk)
-        for k in todo[step * each : (step + 1) * each]:
-            plane_pass(k)
-    for k in todo[(line - 1) * each :]:
-        plane_pass(k)
+            relay(k, piece)
+        pair_copy(k, piece, slot).start()
+
+    todo = [(k, piece) for k in range(1, len(hops)) for piece in range(PIECES)]
+    turns = (line - 1) * CHUNKS
+    due = [1 + e * max(turns - CHUNKS + 1, 0) // max(len(todo), 1) for e in range(len(todo))]
+    for turn in range(turns):
+        step, chunk = turn // CHUNKS, turn % CHUNKS
+        for up in (True, False):
+            line_arrive(up, step, chunk)
+            if step + 1 < line - 1:
+                line_start(up, step + 1, chunk)
+        for event, when in zip(todo, due):
+            if when == turn:
+                plane_pass(*event)
+    for event, when in zip(todo, due):
+        if when >= turns:
+            plane_pass(*event)
     for k in range(len(hops)):
-        pair_copy(k, source(k, partner)).wait_recv()
+        for piece in range(PIECES):
+            pair_copy(k, piece, source(k, partner)).wait_recv()
 
     sharpness = SHARP * math.sqrt(dim)
     count = line * segments
@@ -235,9 +245,10 @@
     for k in range(1, near * wide):
         part_copy(k).wait_send()
     for k in range(len(hops)):
-        if k:
-            own_copy(k, me, hop_to(k)).wait_send()
-        pair_copy(k, source(k, col)).wait_send()
+        for piece in range(PIECES):
+            if k:
+                own_copy(k, piece, me, hop_to(k)).wait_send()
+            pair_copy(k, piece, source(k, col)).wait_send()
     for step in range(line - 1):
         for chunk in range(CHUNKS):
             for up in (True, False):
@@ -276,10 +287,10 @@
             pltpu.VMEM((plane, segments, width - base), jnp.bfloat16),
             dma((2, steps, CHUNKS)),
             dma((2, steps, CHUNKS)),
-            dma((hops,)),
-            dma((hops,)),
-            dma((hops,)),
-            dma((hops,)),
+            dma((hops, PIECES)),
+            dma((hops, PIECES)),
+            dma((hops, PIECES)),
+            dma((hops, PIECES)),
             dma((plane,)),
             dma((plane,)),
         ],

time: 24 us -> 23.5 us (0.979)
  Pallas kernels: 22.3 us -> 21.8 us
    pallas_call x1, Pallas kernels: 22.3 us -> 21.8 us  [shards(): pl.pallas_call(functools.partial(kernel, (line, near, wide, width)), out_...]
where the time goes in v4:
time: 23.5 us; the launch traced here: 23.2 us
  Pallas kernels  21.8 us (93%)
  local copies, waits for them, and re-layouts  1.32 us (6%)
    pallas_call x1, Pallas kernels, shards(): pl.pallas_call(functools.partial(kernel, (line, near, wide, width)), out_...  21.8 us
    unnamed x1, local copies, waits for them, and re-layouts  1.32 us

profile of v4, /device:TPU:0, one launch (start us, length us, event | category | flops | bytes accessed | tf_op | source)
XLA Modules:
  0.0 23.2 jit_solution(16851112446038428075)
XLA Ops:
  0.0 21.8 %shard_map.37 = f32[32,64]{1,0:T(8,128)} custom-call(bf16[5,64,192]{2,1,0:T(8,128)(2,1)} %bitcast.1, f32[5]{0:T(128)} %scale_ref.1, bf16[32,64]{1,0:T(8,128)(2,1)} %vec_ref.1), custom_call_target="tpu_custom_call" | custom-call | tf_op jit(solution)/shard_map/pallas_call | solution.py:272
  21.9 1.3 %copy.5 = f32[32,64]{1,0:T(8,128)} copy(f32[32,64]{1,0:T(8,128)} %shard_map.37) | data formatting | bytes 16384

commit v5 on v4

--- a/solution.py
+++ b/solution.py
@@ -184,6 +184,7 @@
 
     sharpness = SHARP * math.sqrt(dim)
     count = line * segments
+    span = width - feats
     columns = cols[...].reshape(count, width)
     base = feats // LANES * LANES
     tail = columns[:, base:]
@@ -206,9 +207,11 @@
             affinity.astype(jnp.bfloat16), tail, (((1,), (0,)), ((), ())),
             preferred_element_type=jnp.float32,
         )
-        partial[pl.ds(first, wide)] = sums.astype(jnp.bfloat16).reshape(wide, segments, width - base)
-
-        for dc in range(wide):
+        sums = sums[:, feats - base :].reshape(wide, segments, span)
+        sums = jnp.concatenate([sums[:, : segments // 2], sums[:, segments // 2 :]], axis=2)
+        partial[pl.ds(first, wide)] = sums.astype(jnp.bfloat16)
+
+        for dc in reversed(range(wide)):
             dq = step % near
             if dq or dc:
                 k = dq * wide + dc
@@ -238,9 +241,8 @@
     for k in range(1, near * wide):
         part_copy(k).wait_recv()
         total = total + landed[k].astype(jnp.float32)
-    total = total.T
-    low = feats - base
-    out_ref[...] = total[low : low + vecs] / total[low + vecs : low + vecs + 1]
+    total = jnp.concatenate([total[:, :span], total[:, span:]], axis=0).T
+    out_ref[...] = total[:vecs] / total[vecs : vecs + 1]
 
     for k in range(1, near * wide):
         part_copy(k).wait_send()
@@ -265,7 +267,6 @@
     feats = scales * dim
     width = -(-(feats + vecs + 1) // LANES) * LANES
     plane = near * wide
-    base = feats // LANES * LANES
     hops = near * wide // CORES
     steps = max(line - 1, 1)
     dma = pltpu.SemaphoreType.DMA
@@ -283,8 +284,8 @@
             dma,
             pltpu.VMEM((plane, segments, width), jnp.bfloat16),
             pltpu.VMEM((line, segments, width), jnp.bfloat16),
-            pltpu.VMEM((plane, segments, width - base), jnp.bfloat16),
-            pltpu.VMEM((plane, segments, width - base), jnp.bfloat16),
+            pltpu.VMEM((plane, segments // 2, 2 * (width - feats)), jnp.bfloat16),
+            pltpu.VMEM((plane, segments // 2, 2 * (width - feats)), jnp.bfloat16),
             dma((2, steps, CHUNKS)),
             dma((2, steps, CHUNKS)),
             dma((hops, PIECES)),

time: 23.5 us -> 23.5 us (level)
  no operation moved by 1% of the time
where the time goes in v5:
time: 23.5 us; the launch traced here: 23.2 us
  Pallas kernels  21.9 us (93%)
  local copies, waits for them, and re-layouts  1.32 us (6%)
    pallas_call x1, Pallas kernels, shards(): pl.pallas_call(functools.partial(kernel, (line, near, wide, width)), out_...  21.9 us
    unnamed x1, local copies, waits for them, and re-layouts  1.32 us

profile of v5, /device:TPU:0, one launch (start us, length us, event | category | flops | bytes accessed | tf_op | source)
XLA Modules:
  0.0 23.2 jit_solution(9688037278711980008)
XLA Ops:
  0.0 21.9 %shard_map.37 = f32[32,64]{1,0:T(8,128)} custom-call(bf16[5,64,192]{2,1,0:T(8,128)(2,1)} %bitcast.1, f32[5]{0:T(128)} %scale_ref.1, bf16[32,64]{1,0:T(8,128)(2,1)} %vec_ref.1), custom_call_target="tpu_custom_call" | custom-call | tf_op jit(solution)/shard_map/pallas_call | solution.py:273
  21.9 1.3 %copy.5 = f32[32,64]{1,0:T(8,128)} copy(f32[32,64]{1,0:T(8,128)} %shard_map.37) | data formatting | bytes 16384

commit v6 on v4

--- a/solution.py
+++ b/solution.py
@@ -240,7 +240,7 @@
         total = total + landed[k].astype(jnp.float32)
     total = total.T
     low = feats - base
-    out_ref[...] = total[low : low + vecs] / total[low + vecs : low + vecs + 1]
+    out_ref[...] = total[low : low + out_ref.shape[0]]
 
     for k in range(1, near * wide):
         part_copy(k).wait_send()
@@ -269,9 +269,9 @@
     hops = near * wide // CORES
     steps = max(line - 1, 1)
     dma = pltpu.SemaphoreType.DMA
-    return pl.pallas_call(
+    sums = pl.pallas_call(
         functools.partial(kernel, (line, near, wide, width)),
-        out_shape=jax.ShapeDtypeStruct((vecs, segments), jnp.float32),
+        out_shape=jax.ShapeDtypeStruct((width - feats, segments), jnp.float32),
         in_specs=[
             pl.BlockSpec(memory_space=pl.ANY),
             pl.BlockSpec(memory_space=pltpu.SMEM),
@@ -298,6 +298,7 @@
             collective_id=0, has_side_effects=True, vmem_limit_bytes=56 * 1024 * 1024
         ),
     )(jnp.swapaxes(embeddings, 1, 2), scale_weights, vectors)
+    return sums[:vecs] / sums[vecs : vecs + 1]
 
 
 def solution(mesh):

time: 23.5 us -> 24.2 us (1.030)
  other arithmetic: 0 us -> 1.33 us
  local copies, waits for them, and re-layouts: 1.32 us -> 0.67 us
    div x0 -> x1, other arithmetic: none -> 1.33 us  [shards(): return sums[:vecs] / sums[vecs:vecs + 1]]
    unnamed x1 -> x0, local copies, waits for them, and re-layouts: 1.32 us -> none
    div x0 -> x1, local copies, waits for them, and re-layouts: none -> 0.67 us  [shards(): return sums[:vecs] / sums[vecs:vecs + 1]]
where the time goes in v6:
time: 24.2 us; the launch traced here: 23.9 us
  Pallas kernels  21.8 us (90%)
  other arithmetic  1.33 us (5%)
  local copies, waits for them, and re-layouts  0.67 us (3%)
    pallas_call x1, Pallas kernels, shards(): pl.pallas_call(functools.partial(kernel, (line, near, wide, width)), out_...  21.8 us
    div x1, other arithmetic, shards(): return sums[:vecs] / sums[vecs:vecs + 1]  1.33 us
    div x1, local copies, waits for them, and re-layouts, shards(): return sums[:vecs] / sums[vecs:vecs + 1]  0.67 us

profile of v6, /device:TPU:0, one launch (start us, length us, event | category | flops | bytes accessed | tf_op | source)
XLA Modules:
  0.0 23.9 jit_solution(16452010583248338576)
XLA Ops:
  0.0 21.8 %shard_map.37 = f32[64,64]{1,0:T(8,128)} custom-call(bf16[5,64,192]{2,1,0:T(8,128)(2,1)} %bitcast.3, f32[5]{0:T(128)} %scale_ref.1, bf16[32,64]{1,0:T(8,128)(2,1)} %vec_ref.1), custom_call_target="tpu_custom_call" | custom-call | tf_op jit(solution)/shard_map/pallas_call | solution.py:272
  21.9 0.7 %slice_bitcast_fusion = f32[64]{0:T(128)S(1)} fusion(f32[64,64]{1,0:T(8,128)} %shard_map.37), kind=kLoop, calls=%fused_computation.1 | loop fusion | bytes 512 | tf_op jit(solution)/shard_map/div | solution.py:301
  22.5 1.3 %slice_divide_fusion = f32[32,64]{1,0:T(8,128)} fusion(f32[64,64]{1,0:T(8,128)} %shard_map.37, f32[64]{0:T(128)S(1)} %slice_bitcast_fusion), kind=kLoop, calls=%fused_computation | loop fusion | flops 2048 | bytes 16640 | tf_op jit(solution)/shard_map/div | solution.py:301
